TPU v7x, 32 devices: a whole 2x2x4 slice. The times are simulated.
32 devices in a mesh: row: 4 (over z), col: 8 (over y, x, core).
Axes of the slice: x: 2, y: 2, z: 4, core: 2. Of those that a mesh axis runs over, the one named last changes fastest.
Arguments:
- initial: bfloat16 [8, 24576], P(None, ('row', 'col')), may hold values from -8 to 8
- matrix: bfloat16 [24576, 24576], P('row', 'col'), may hold values from -1 to 4, as said below
Outputs:
- vectors: float32 [8, 24576], P(None, ('row', 'col'))
- estimates: float32 [4, 8], replicated
Inputs may be any that keep to these rules, and one draw needn't show every extreme that they name: matrix is symmetric: entry (i, j) equals entry (j, i).
All inputs are finite; a program needn't handle non-finite values.
Results may differ from a plain program's by a relative error of at most 0.008.
Values may be sent and summed in bfloat16 or wider, within the bound.
A program may use at most 64 MiB of HBM per device.

v0:
```python
import functools

import jax
import jax.numpy as jnp
from jax import lax
from jax.experimental import pallas as pl
from jax.experimental.pallas import tpu as pltpu
from jax.sharding import PartitionSpec as P

ITERS = 4
MESH = pl.DeviceIdType.MESH
LANES = 128


def exchange(n, reduce_rows, last, rows, cols, x_ref, out_ref, est_ref, parts, full, grams,
             send1, recv1, send2, recv2, send3, recv3):
    r = lax.axis_index("row")
    c = lax.axis_index("col")
    total = rows * cols
    flat = r * cols + c
    me = r if reduce_rows else c
    k_vec = x_ref.shape[0]
    chunk = x_ref.shape[1] // n

    def member(j):
        return (j, c) if reduce_rows else (r, j)

    def device(i):
        return (i // cols, lax.rem(i, cols))

    barrier = pltpu.get_barrier_semaphore()
    for k in range(1, total):
        pl.semaphore_signal(
            barrier, inc=1, device_id=device(lax.rem(flat + k, total)), device_id_type=MESH
        )
    pl.semaphore_wait(barrier, total - 1)

    scatter = []
    for k in range(1, n):
        to = lax.rem(me + k, n)
        copy = pltpu.make_async_remote_copy(
            src_ref=x_ref.at[:, pl.ds(pl.multiple_of(to * chunk, LANES), chunk)],
            dst_ref=parts.at[k - 1],
            send_sem=send1.at[k - 1],
            recv_sem=recv1.at[k - 1],
            device_id=member(to),
            device_id_type=MESH,
        )
        copy.start()
        scatter.append(copy)
    summed = x_ref[:, pl.ds(pl.multiple_of(me * chunk, LANES), chunk)]
    for k in range(1, n):
        scatter[k - 1].wait_recv()
        summed = summed + parts[k - 1]

    gather = []
    if not last:
        full[me] = summed
        for k in range(1, n):
            copy = pltpu.make_async_remote_copy(
                src_ref=full.at[me],
                dst_ref=full.at[me],
                send_sem=send2.at[k - 1],
                recv_sem=recv2.at[k - 1],
                device_id=member(lax.rem(me + k, n)),
                device_id_type=MESH,
            )
            gather.append(copy)

    lane = lax.broadcasted_iota(jnp.int32, (k_vec, LANES), 1)
    sub = lax.broadcasted_iota(jnp.int32, (k_vec, LANES), 0)
    gram = jnp.zeros((k_vec, LANES), jnp.float32)
    for k in range(k_vec):
        column = jnp.sum(summed * summed[k:k + 1, :], axis=1, keepdims=True)
        gram = jnp.where(lane == k, column, gram)
    grams[flat] = gram
    share = []
    for k in range(1, total):
        copy = pltpu.make_async_remote_copy(
            src_ref=grams.at[flat],
            dst_ref=grams.at[flat],
            send_sem=send3.at[k - 1],
            recv_sem=recv3.at[k - 1],
            device_id=device(lax.rem(flat + k, total)),
            device_id_type=MESH,
        )
        copy.start()
        share.append(copy)
    for copy in gather:
        copy.start()
    for copy in share:
        copy.wait_recv()
    gram = grams[0]
    for k in range(1, total):
        gram = gram + grams[k]

    work = jnp.where(lane - k_vec == sub, 1.0, gram)
    est = jnp.zeros((k_vec, LANES), jnp.float32)
    scale = jnp.zeros((k_vec, LANES), jnp.float32)
    for k in range(k_vec):
        row = work[k:k + 1, :]
        pivot = row[:, k:k + 1]
        root = jnp.sqrt(pivot)
        est = jnp.where(lane == k, root, est)
        scale = jnp.where(sub == k, 1.0 / root, scale)
        factor = jnp.where(sub > k, work[:, k:k + 1] / pivot, 0.0)
        work = work - factor * row
    est_ref[...] = est
    inverse = work * scale
    columns = [inverse[:, k_vec + k:k_vec + k + 1] for k in range(k_vec)]

    def apply(block):
        result = columns[0] * block[0:1, :]
        for k in range(1, k_vec):
            result = result + columns[k] * block[k:k + 1, :]
        return result

    if last:
        out_ref[...] = apply(summed)
    else:
        for copy in gather:
            copy.wait_recv()
        for j in range(n):
            out_ref[:, j * chunk:(j + 1) * chunk] = apply(full[j]).astype(out_ref.dtype)
    for copy in scatter + gather + share:
        copy.wait_send()


def normalise(partial_sum, reduce_rows, last, collective_id):
    rows, cols = lax.axis_size("row"), lax.axis_size("col")
    n = rows if reduce_rows else cols
    k_vec, width = partial_sum.shape
    held = width // n
    chunk = pl.cdiv(held, LANES) * LANES
    padded = chunk != held
    if padded:
        partial_sum = jnp.pad(
            partial_sum.reshape(k_vec, n, held), ((0, 0), (0, 0), (0, chunk - held))
        ).reshape(k_vec, n * chunk)
    total = rows * cols
    if last:
        out = jax.ShapeDtypeStruct((k_vec, chunk), jnp.float32)
    else:
        out = jax.ShapeDtypeStruct((k_vec, n * chunk), jnp.bfloat16)
    dma = pltpu.SemaphoreType.DMA
    updated, est = pl.pallas_call(
        functools.partial(exchange, n, reduce_rows, last, rows, cols),
        out_shape=(out, jax.ShapeDtypeStruct((k_vec, LANES), jnp.float32)),
        in_specs=[pl.BlockSpec(memory_space=pltpu.VMEM)],
        out_specs=(pl.BlockSpec(memory_space=pltpu.VMEM),) * 2,
        scratch_shapes=[
            pltpu.VMEM((n - 1, k_vec, chunk), jnp.float32),
            pltpu.VMEM((n, k_vec, chunk), jnp.float32),
            pltpu.VMEM((total, k_vec, LANES), jnp.float32),
            dma((n - 1,)), dma((n - 1,)),
            dma((n - 1,)), dma((n - 1,)),
            dma((total - 1,)), dma((total - 1,)),
        ],
        compiler_params=pltpu.CompilerParams(
            collective_id=collective_id, has_side_effects=True
        ),
    )(partial_sum)
    if padded:
        updated = updated.reshape(k_vec, -1, chunk)[:, :, :held].reshape(k_vec, -1)
    return updated, est


def shards(initial, matrix):
    diagonals = []
    current = lax.all_gather(initial, "col", axis=1, tiled=True)
    for iteration in range(ITERS):
        reduce_rows = iteration % 2 == 0
        last = iteration == ITERS - 1
        contract = ((1,), (0,)) if reduce_rows else ((1,), (1,))
        partial_sum = lax.dot_general(
            current, matrix, (contract, ((), ())), preferred_element_type=jnp.float32
        )
        current, est = normalise(
            partial_sum, reduce_rows, last, 2 if last else (0 if reduce_rows else 1)
        )
        diagonals.append(est[0, :initial.shape[0]])
    return (current, jnp.stack(diagonals))


def solution(mesh):
    return jax.shard_map(
        shards,
        mesh=mesh,
        in_specs=(P(None, ("row", "col")), P("row", "col")),
        out_specs=(P(None, ("row", "col")), P()),
        check_vma=False,
    )
```

profile of v0, /device:TPU:0, one launch (start us, length us, event | category | flops | bytes accessed | tf_op | source)
XLA Modules:
  0.0 144.4 jit_solution(18123580381714221561)
XLA Ops:
  0.6 10.9 %all_gather.3 = bf16[8,6144]{1,0:T(8,128)(2,1)S(1)} all-gather(bf16[8,768]{1,0:T(8,128)(2,1)} %param.2), channel_id=1, replica_groups=mesh['row'=4,'col'=8] {'col'}, dimensions={1}, use_global_device_ids=true | all-gather | bytes 110592 | tf_op jit(solution)/shard_map/all_gather | solution.py:170
  11.5 14.9 %fusion.x_ref = f32[8,3072]{1,0:T(8,128)} fusion(bf16[8,6144]{1,0:T(8,128)(2,1)S(1)} %all_gather.3, bf16[6144,3072]{1,0:T(8,128)(2,1)} %param.3), kind=kOutput, calls=%fused_computation.1 | convolution fusion | flops 301989888 | bytes 37945344 | tf_op jit(solution)/shard_map/dot_general | solution.py:175
  26.4 16.6 %shard_map.41 = (bf16[8,3072]{1,0:T(8,128)(2,1)}, f32[8,128]{1,0:T(8,128)}) custom-call(f32[8,3072]{1,0:T(8,128)} %fusion.x_ref), custom_call_target="tpu_custom_call" | custom-call | tf_op jit(solution)/shard_map/pallas_call | solution.py:146
  43.0 0.7 slice.12
  43.7 16.6 %fusion.1.x_ref = f32[8,6144]{1,0:T(8,128)} fusion(bf16[8,3072]{1,0:T(8,128)(2,1)} %get-tuple-element.10, bf16[6144,3072]{1,0:T(8,128)(2,1)} %param.3), kind=kOutput, calls=%fused_computation.2 | convolution fusion | flops 301989888 | bytes 37994496 | tf_op jit(solution)/shard_map/dot_general | solution.py:175
  60.2 16.9 %shard_map.42 = (bf16[8,6144]{1,0:T(8,128)(2,1)}, f32[8,128]{1,0:T(8,128)}) custom-call(f32[8,6144]{1,0:T(8,128)} %fusion.1.x_ref), custom_call_target="tpu_custom_call" | custom-call | tf_op jit(solution)/shard_map/pallas_call | solution.py:146
  77.2 14.9 %fusion.2.x_ref = f32[8,3072]{1,0:T(8,128)} fusion(bf16[8,6144]{1,0:T(8,128)(2,1)} %get-tuple-element.11, bf16[6144,3072]{1,0:T(8,128)(2,1)} %param.3), kind=kOutput, calls=%fused_computation.3 | convolution fusion | flops 301989888 | bytes 37945344 | tf_op jit(solution)/shard_map/dot_general | solution.py:175
  92.1 15.8 %shard_map.43 = (bf16[8,3072]{1,0:T(8,128)(2,1)}, f32[8,128]{1,0:T(8,128)}) custom-call(f32[8,3072]{1,0:T(8,128)} %fusion.2.x_ref), custom_call_target="tpu_custom_call" | custom-call | tf_op jit(solution)/shard_map/pallas_call | solution.py:146
  108.0 0.7 slice.14
  108.7 0.7 slice.13
  109.3 16.6 %fusion.3.x_ref = f32[8,6144]{1,0:T(8,128)} fusion(bf16[8,3072]{1,0:T(8,128)(2,1)} %get-tuple-element.12, bf16[6144,3072]{1,0:T(8,128)(2,1)} %param.3), kind=kOutput, calls=%fused_computation.4 | convolution fusion | flops 301989888 | bytes 37994496 | tf_op jit(solution)/shard_map/dot_general | solution.py:175
  125.9 15.9 %shard_map.44 = (f32[8,768]{1,0:T(8,128)}, f32[8,128]{1,0:T(8,128)}) custom-call(f32[8,6144]{1,0:T(8,128)} %fusion.3.x_ref), custom_call_target="tpu_custom_call" | custom-call | tf_op jit(solution)/shard_map/pallas_call | solution.py:146
  141.8 0.7 slice.15
  142.5 0.6 pad_maximum_fusion
  143.1 1.3 copy.5
where the time goes:
time: 145 us; the launch traced here: 144 us
  Pallas kernels  65.2 us (45%)
  matrix products  63 us (43%)
  blocking collectives  10.9 us (8%)
  local copies, waits for them, and re-layouts  4.06 us (3%)
    pallas_call x4, Pallas kernels, normalise(): pl.pallas_call(functools.partial(exchange, n, reduce_rows, last, rows, co...  65.2 us
    dot_general x4, matrix products, shards(): lax.dot_general(current, matrix, (contract, ((), ())), preferred_element_...  63 us
    all_gather x1, blocking collectives, shards(): current = lax.all_gather(initial, 'col', axis=1, tiled=True)  10.9 us

commit v1 on v0

--- a/solution.py
+++ b/solution.py
@@ -10,6 +10,7 @@
 ITERS = 4
 MESH = pl.DeviceIdType.MESH
 LANES = 128
+LIMBS = 2
 
 
 def exchange(n, reduce_rows, last, rows, cols, x_ref, out_ref, est_ref, parts, full, grams,
@@ -182,9 +183,279 @@
     return (current, jnp.stack(diagonals))
 
 
+def update(work, k_vec, lane, sub):
+    work = jnp.where(lane - k_vec == sub, 1.0, work)
+    est = jnp.zeros((k_vec, LANES), jnp.float32)
+    scale = jnp.zeros((k_vec, LANES), jnp.float32)
+    for k in range(k_vec):
+        row = work[k:k + 1, :]
+        pivot = row[:, k:k + 1]
+        root = jnp.sqrt(pivot)
+        est = jnp.where(lane == k, root, est)
+        scale = jnp.where(sub == k, 1.0 / root, scale)
+        factor = jnp.where(sub > k, work[:, k:k + 1] / pivot, 0.0)
+        work = work - factor * row
+    inverse = work * scale
+    return est, [inverse[:, k_vec + k:k_vec + k + 1] for k in range(k_vec)]
+
+
+def fused(rows, cols, steps, first_ref, matrix_ref, out_ref, est_ref,
+          mat, start, opened, block, early, ship, landed, full, grams, mine,
+          load_sem, s0, r0, s1, r1, s2, r2, s3, r3):
+    r = lax.axis_index("row")
+    c = lax.axis_index("col")
+    total = rows * cols
+    flat = r * cols + c
+    k_vec, held = first_ref.shape
+    height, width = mat.shape
+    piece = height // steps
+
+    def device(i):
+        return (i // cols, lax.rem(i, cols))
+
+    def span(j, size):
+        return pl.ds(pl.multiple_of(j * size, LANES), size)
+
+    def load(i, p):
+        window = (pl.ds(p * piece, piece), span(lax.rem(r + i, rows), held))
+        return pltpu.make_async_copy(
+            matrix_ref.at[window], mat.at[window], load_sem.at[(i - 1) * steps + p]
+        )
+
+    for i in range(1, rows + 1):
+        for p in range(steps):
+            load(i, p).start()
+
+    barrier = pltpu.get_barrier_semaphore()
+
+    def greet(k, carry):
+        pl.semaphore_signal(
+            barrier, inc=1, device_id=device(lax.rem(flat + k, total)), device_id_type=MESH
+        )
+        return carry
+
+    lax.fori_loop(1, total, greet, 0)
+    pl.semaphore_wait(barrier, total - 1)
+
+    def opening(k):
+        return pltpu.make_async_remote_copy(
+            src_ref=first_ref, dst_ref=start.at[c], send_sem=s0.at[k - 1], recv_sem=r0.at[k - 1],
+            device_id=(r, lax.rem(c + k, cols)), device_id_type=MESH,
+        )
+
+    for k in range(1, cols):
+        opening(k).start()
+    start[c] = first_ref[...]
+    for k in range(1, cols):
+        opening(k).wait_recv()
+    for j in range(cols):
+        opened[:, j * held:(j + 1) * held] = start[j]
+
+    lane = lax.broadcasted_iota(jnp.int32, (k_vec, LANES), 1)
+    sub = lax.broadcasted_iota(jnp.int32, (k_vec, LANES), 0)
+
+    def split(slot, rest):
+        for limb in range(LIMBS):
+            part = rest.astype(block.dtype)
+            block[slot, limb * k_vec:(limb + 1) * k_vec, :] = part
+            rest = rest - part.astype(jnp.float32)
+
+    unsent = []
+    previous = None
+
+    def fold(value):
+        result = value[:k_vec]
+        for limb in range(1, LIMBS):
+            result = result + value[limb * k_vec:(limb + 1) * k_vec]
+        return result
+
+    def share(t, k):
+        return pltpu.make_async_remote_copy(
+            src_ref=mine.at[t], dst_ref=grams.at[t, k - 1], send_sem=s3.at[t], recv_sem=r3.at[t],
+            device_id=device(lax.rem(flat + k, total)), device_id_type=MESH,
+        )
+
+    def arrival(t):
+        everyone = grams.at[t, pl.ds(0, total - 1)]
+        return pltpu.make_async_remote_copy(
+            src_ref=everyone, dst_ref=everyone, send_sem=s3.at[t], recv_sem=r3.at[t],
+            device_id=device(flat), device_id_type=MESH,
+        )
+
+    def inverse(t):
+        arrival(t).wait_recv()
+        spread = jnp.broadcast_to(mine[t] + jnp.sum(grams[t], axis=0), (k_vec, LANES))
+        gram = jnp.zeros((k_vec, LANES), jnp.float32)
+        for k in range(k_vec):
+            column = jnp.sum(jnp.where(lane == k_vec * sub + k, spread, 0.0), axis=1, keepdims=True)
+            gram = jnp.where(lane == k, column, gram)
+        est, columns = update(gram, k_vec, lane, sub)
+        est_ref[t:t + 1, :] = est[0:1, :k_vec]
+        return columns
+
+    def apply(columns, value):
+        result = columns[0] * value[0:1, :]
+        for k in range(1, k_vec):
+            result = result + columns[k] * value[k:k + 1, :]
+        return result
+
+    for t in range(ITERS):
+        down = t % 2 == 0
+        last = t == ITERS - 1
+        n = rows if down else cols
+        me = r if down else c
+
+        def member(j, down=down):
+            return (j, c) if down else (r, j)
+
+        def scatter(i, t=t, n=n, me=me, member=member):
+            return pltpu.make_async_remote_copy(
+                src_ref=ship.at[t, i - 1], dst_ref=landed.at[t, i - 1],
+                send_sem=s1.at[t, i - 1], recv_sem=r1.at[t, i - 1],
+                device_id=member(lax.rem(me + i, n)), device_id_type=MESH,
+            )
+
+        def gather(i, t=t, n=n, me=me, member=member):
+            return pltpu.make_async_remote_copy(
+                src_ref=full.at[t, me], dst_ref=full.at[t, me],
+                send_sem=s2.at[t, i - 1], recv_sem=r2.at[t, i - 1],
+                device_id=member(lax.rem(me + i, n)), device_id_type=MESH,
+            )
+
+        def terms(i, slots, t=t, down=down, n=n, me=me):
+            j = lax.rem(me + i, n)
+            m, mine_at = (cols, c) if down else (rows, r)
+            acc = None
+            for slot in slots:
+                k = lax.rem(mine_at + slot, m)
+                if down:
+                    term = jnp.dot(block[slot], mat[span(k, held), span(j, held)],
+                                   preferred_element_type=jnp.float32)
+                else:
+                    term = lax.dot_general(
+                        block[slot], mat[span(j, held), span(k, held)], (((1,), (1,)), ((), ())),
+                        preferred_element_type=jnp.float32)
+                acc = term if acc is None else acc + term
+            return fold(acc)
+
+        def product(i, t=t, down=down, n=n, me=me, terms=terms):
+            if t > 0:
+                return early[i - 1] + terms(i, range(1, cols if down else rows))
+            j = lax.rem(me + i, n)
+            for p in range(steps):
+                window = pl.ds(p * piece, piece)
+                pltpu.make_async_copy(
+                    matrix_ref.at[window, pl.ds(0, held)], mat.at[window, pl.ds(0, held)],
+                    load_sem.at[(i - 1) * steps + p],
+                ).wait()
+            return jnp.dot(opened[...], mat[:, span(j, held)],
+                           preferred_element_type=jnp.float32)
+
+        if t > 0:
+            def ahead(i, carry, terms=terms):
+                early[i - 1] = terms(i, range(1))
+                return carry
+
+            lax.fori_loop(1, n + 1, ahead, 0, unroll=4)
+            for i in range(1, previous[0]):
+                previous[2](i).wait_recv()
+            for slot in range(1, previous[0]):
+                split(slot, full[t - 1, lax.rem(previous[1] + slot, previous[0])])
+
+        def step(i, carry, t=t, product=product, scatter=scatter):
+            ship[t, i - 1] = product(i)
+            scatter(i).start()
+            return carry
+
+        lax.fori_loop(1, n, step, 0)
+        summed = product(n)
+        if t > 0:
+            columns = inverse(t - 1)
+        for i in range(1, n):
+            scatter(i).wait_recv()
+            summed = summed + landed[t, i - 1]
+        if t > 0:
+            summed = apply(columns, summed)
+
+        if not last:
+            full[t, me] = summed
+            for i in range(1, n):
+                gather(i).start()
+        row = jnp.zeros((k_vec, LANES), jnp.float32)
+        for k in range(k_vec):
+            column = jnp.sum(summed * summed[k:k + 1, :], axis=1, keepdims=True)
+            row = jnp.where(lane == k_vec * sub + k, column, row)
+        mine[t] = jnp.sum(row, axis=0, keepdims=True)
+
+        def shares(k, carry, t=t):
+            share(t, k).start()
+            return carry
+
+        lax.fori_loop(1, total, shares, 0)
+        if last:
+            out_ref[...] = apply(inverse(t), summed)
+        else:
+            split(0, summed)
+            previous = (n, me, gather)
+        unsent += [scatter(i) for i in range(1, n)]
+        if not last:
+            unsent += [gather(i) for i in range(1, n)]
+    for copy in unsent:
+        copy.wait_send()
+    for t in range(ITERS):
+        arrival(t).wait_send()
+    for k in range(1, cols):
+        opening(k).wait_send()
+
+
+def whole(initial, matrix):
+    rows, cols = lax.axis_size("row"), lax.axis_size("col")
+    k_vec, held = initial.shape
+    height, width = matrix.shape
+    total = rows * cols
+    most = max(rows, cols)
+    steps = 4
+    dma = pltpu.SemaphoreType.DMA
+    return pl.pallas_call(
+        functools.partial(fused, rows, cols, steps),
+        out_shape=(jax.ShapeDtypeStruct((k_vec, held), jnp.float32),
+                   jax.ShapeDtypeStruct((ITERS, k_vec), jnp.float32)),
+        in_specs=[pl.BlockSpec(memory_space=pltpu.VMEM), pl.BlockSpec(memory_space=pl.ANY)],
+        out_specs=(pl.BlockSpec(memory_space=pltpu.VMEM),) * 2,
+        scratch_shapes=[
+            pltpu.VMEM((height, width), matrix.dtype),
+            pltpu.VMEM((cols, k_vec, held), initial.dtype),
+            pltpu.VMEM((k_vec, height), initial.dtype),
+            pltpu.VMEM((most, LIMBS * k_vec, held), initial.dtype),
+            pltpu.VMEM((most, k_vec, held), jnp.float32),
+            pltpu.VMEM((ITERS, most - 1, k_vec, held), jnp.float32),
+            pltpu.VMEM((ITERS, most - 1, k_vec, held), jnp.float32),
+            pltpu.VMEM((ITERS, most, k_vec, held), jnp.float32),
+            pltpu.VMEM((ITERS, total - 1, 1, LANES), jnp.float32),
+            pltpu.VMEM((ITERS, 1, LANES), jnp.float32),
+            dma((rows * steps,)),
+            dma((cols - 1,)), dma((cols - 1,)),
+            dma((ITERS, most - 1)), dma((ITERS, most - 1)),
+            dma((ITERS, most - 1)), dma((ITERS, most - 1)),
+            dma((ITERS,)), dma((ITERS,)),
+        ],
+        compiler_params=pltpu.CompilerParams(
+            collective_id=0, has_side_effects=True, vmem_limit_bytes=60 * 2**20
+        ),
+    )(initial, matrix)
+
+
+def program(initial, matrix):
+    k_vec, held = initial.shape
+    resident = matrix.size * matrix.dtype.itemsize <= 40 * 2**20
+    if held % LANES == 0 and k_vec * k_vec <= LANES and resident:
+        return whole(initial, matrix)
+    return shards(initial, matrix)
+
+
 def solution(mesh):
     return jax.shard_map(
-        shards,
+        program,
         mesh=mesh,
         in_specs=(P(None, ("row", "col")), P("row", "col")),
         out_specs=(P(None, ("row", "col")), P()),

time: 145 us -> 68.2 us (0.47)
  matrix products: 63 us -> 0 us
  blocking collectives: 10.9 us -> 0 us
  local copies, waits for them, and re-layouts: 4.06 us -> 2.59 us
    dot_general x4 -> x0, matrix products: 63 us -> none  [shards(): lax.dot_general(current, matrix, (contract, ((), ())), preferred_element_...]
    all_gather x1 -> x0, blocking collectives: 10.9 us -> none  [shards(): current = lax.all_gather(initial, 'col', axis=1, tiled=True)]
    slice x4 -> x0, local copies, waits for them, and re-layouts: 2.71 us -> none  [shards(): diagonals.append(est[0, :initial.shape[0]])]
    pallas_call x4 -> x1, Pallas kernels: 65.2 us -> 64.7 us  [whole(): pl.pallas_call(functools.partial(fused, rows, cols, steps), out_shape=(ja...]
where the time goes in v1:
time: 68.2 us; the launch traced here: 67.9 us
  Pallas kernels  64.7 us (95%)
  local copies, waits for them, and re-layouts  2.59 us (4%)
    pallas_call x1, Pallas kernels, whole(): pl.pallas_call(functools.partial(fused, rows, cols, steps), out_shape=(ja...  64.7 us
    unnamed x2, local copies, waits for them, and re-layouts  2.59 us

profile of v1, /device:TPU:0, one launch (start us, length us, event | category | flops | bytes accessed | tf_op | source)
XLA Modules:
  0.0 67.9 jit_solution(5556081203874117619)
XLA Ops:
  0.6 64.7 %shard_map.41 = (f32[8,768]{1,0:T(8,128)}, f32[4,8]{1,0:T(4,128)}) custom-call(bf16[8,768]{1,0:T(8,128)(2,1)} %first_ref.1, bf16[6144,3072]{1,0:T(8,128)(2,1)} %matrix_ref.1), custom_call_target="tpu_custom_call" | custom-call | tf_op jit(solution)/shard_map/pallas_call | solution.py:419
  65.3 1.3 %copy.6 = f32[8,768]{1,0:T(8,128)} copy(f32[8,768]{1,0:T(8,128)} %get-tuple-element.4) | data formatting | bytes 49152
  66.7 1.2 %copy.7 = f32[4,8]{1,0:T(4,128)} copy(f32[4,8]{1,0:T(4,128)} %get-tuple-element.5) | data formatting | bytes 256
